TPU v7x, 32 devices: a 4x4x1 block of a 4x4x8 slice. The times are simulated.
32 devices in a mesh: dp: 1 (over z), tp: 32 (over x, y, core).
Axes of the slice: x: 4, y: 4, z: 1, core: 2. Of those that a mesh axis runs over, the one named last changes fastest.
The devices are a block of a 4x4x8 slice.
Arguments:
- x: bfloat16 [7168, 5120], P(('dp', 'tp'))
- w_gate: bfloat16 [5120, 32768], P(None, 'tp')
- w_up: bfloat16 [5120, 32768], P(None, 'tp')
- w_down: bfloat16 [32768, 5120], P('tp')
Outputs:
- output: bfloat16 [7168, 5120], P(('dp', 'tp'))
All inputs are finite; a program needn't handle non-finite values.
Results may differ from a plain program's by a relative error of at most 0.016.
Values are sent between devices in bfloat16 or wider.
A program may use at most 768 MiB of HBM per device.

v0:
```python
import jax
import jax.numpy as jnp
from jax import lax
from jax.sharding import PartitionSpec as P


def solution(mesh):
    def step(x, w_gate, w_up, w_down):
        rows = lax.all_gather(x, "tp", axis=0, tiled=True)
        gate = jnp.dot(rows, w_gate, preferred_element_type=jnp.float32)
        up = jnp.dot(rows, w_up, preferred_element_type=jnp.float32)
        hidden = (jax.nn.silu(gate) * up).astype(jnp.bfloat16)
        term = jnp.dot(hidden, w_down, preferred_element_type=jnp.float32).astype(jnp.bfloat16)
        return lax.psum_scatter(term, "tp", scatter_dimension=0, tiled=True)

    return jax.shard_map(
        step,
        mesh=mesh,
        in_specs=(P(("dp", "tp"), None), P(None, "tp"), P(None, "tp"), P("tp", None)),
        out_specs=P(("dp", "tp"), None),
        check_vma=False,
    )
```

profile of v0, /device:TPU:96, one launch (start us, length us, event | category | flops | bytes accessed | tf_op | source)
XLA Modules:
  0.0 793.3 jit_solution(10255771181011624300)
XLA Ops:
  6.5 0.0 all-gather.2.cloned.1.call-start
  6.6 0.7 all-gather.2.cloned.1.call-update
  7.3 0.1 reduce-scatter.4.cloned.1.call-start
  7.4 216.8 %all-gather.2.cloned.1.call-done = bf16[7168,5120]{1,0:T(8,128)(2,1)} async-done(((bf16[224,5120]{1,0:T(8,128)(2,1)}), bf16[7168,5120]{1,0:T(8,128)(2,1)}) %all-gather.2.cloned.1.call-update) | async-done | bytes 73400336 | tf_op jit(solution)/shard_map/all_gather | solution.py:9
  224.2 85.7 %fusion = f32[7168,1024]{1,0:T(8,128)} fusion(bf16[7168,5120]{1,0:T(8,128)(2,1)} %all-gather.2.cloned.1.call-done, bf16[5120,1024]{1,0:T(8,128)(2,1)} %param.5), kind=kOutput, calls=%fused_computation.2 | convolution fusion | flops 75161927680 | bytes 113246208 | tf_op jit(solution)/shard_map/dot_general | solution.py:10
  309.9 87.6 %multiply_convert_fusion = bf16[7168,1024]{1,0:T(8,128)(2,1)} fusion(f32[7168,1024]{1,0:T(8,128)} %fusion, bf16[7168,5120]{1,0:T(8,128)(2,1)} %all-gather.2.cloned.1.call-done, bf16[5120,1024]{1,0:T(8,128)(2,1)} %param.6), kind=kOutput, calls=%fused_computation.1 | convolution fusion | flops 75205967872 | bytes 127926272 | tf_op jit(solution)/shard_map/dot_general | solution.py:11
  397.4 85.6 %convolution_convert_fusion = bf16[7168,5120]{1,0:T(8,128)(2,1)} fusion(bf16[7168,1024]{1,0:T(8,128)(2,1)} %multiply_convert_fusion, bf16[1024,5120]{1,0:T(8,128)(2,1)} %param.7), kind=kOutput, calls=%fused_computation | convolution fusion | flops 75198627840 | bytes 98566144 | tf_op jit(solution)/shard_map/dot_general | solution.py:13
  483.0 0.1 reduce-scatter.4.cloned.1.call-update
  483.1 303.3 %reduce-scatter.4.cloned.1.call-done = bf16[224,5120]{1,0:T(8,128)(2,1)} async-done(((bf16[7168,5120]{1,0:T(8,128)(2,1)}), bf16[224,5120]{1,0:T(8,128)(2,1)}) %reduce-scatter.4.cloned.1.call-update) | async-done | bytes 2293776
Async XLA Ops:
  6.5 217.6 %all-gather.2.cloned.1.call-start = ((), (), s32[]{:S(2)}) async-start(), calls=%async_computation.1 | async-start | bytes 75694080 | tf_op jit(solution)/shard_map/all_gather | solution.py:9
  7.3 779.1 %reduce-scatter.4.cloned.1.call-start = ((), (), s32[]{:S(2)}) async-start(), calls=%async_computation.2 | async-start | bytes 75694080
Sparse Core Ops, SparseCore 0:
  9.4 214.7 all-gather.1
  483.2 303.1 reduce-scatter.3
where the time goes:
time: 794 us; the launch traced here: 793 us
  waiting for transfers between devices  521 us (66%)
  matrix products  259 us (33%)
  between operations  13.4 us (2%)
    unnamed x3, waiting for transfers between devices  304 us
    all_gather x1, waiting for transfers between devices, step(): rows = lax.all_gather(x, 'tp', axis=0, tiled=True)  217 us
    dot_general x1, matrix products, step(): up = jnp.dot(rows, w_up, preferred_element_type=jnp.float32)  87.6 us
    dot_general x1, matrix products, step(): gate = jnp.dot(rows, w_gate, preferred_element_type=jnp.float32)  85.7 us
    dot_general x1, matrix products, step(): jnp.dot(hidden, w_down, preferred_element_type=jnp.float32)  85.6 us
  transfers between devices with their start and end apart: 2, of which 2 were waited for; matrix products, arithmetic and copies ran while one was open for 0% of the time, Pallas kernels for 0%

commit v1 on v0

v1 whole, which is shorter than its diff:
```python
import functools
import math

import jax
import jax.numpy as jnp
from jax import lax
from jax.experimental import pallas as pl
from jax.experimental.pallas import tpu as pltpu
from jax.sharding import PartitionSpec as P

MESH = pl.DeviceIdType.MESH
BF16 = jnp.bfloat16
F32 = jnp.float32


def neighbours(tp, side):
    core, chip = tp % 2, tp // 2
    x, y = chip // side, chip % side
    last = ((x + y) % side + 1) // side
    first = (side - (x + y) % side) // side

    def at(u, v):
        return (u * side + v) * 2 + core

    a = (at((x + last) % side, (y + 1 - last) % side), at((x + side - first) % side, (y + side - 1 + first) % side))
    b = (at((x + 1 - last) % side, (y + last) % side), at((x + side - 1 + first) % side, (y + side - first) % side))
    turn = lambda p: (p[0] + core * (p[1] - p[0]), p[1] + core * (p[0] - p[1]))
    return turn(a), turn(b), tp + 1 - 2 * core


def kernel(
    cfg,
    x_ref, wg_ref, wu_ref, wd_ref,
    y_ref, xg_ref, xp_ref,
    wg, wu, wd, xv, hid, run, pt, out, outp,
    w_sem, xv_sem, y_sem, ag_send, ag_recv, xp_send, xp_recv, run_send, run_recv, pt_send, pt_recv, run_free, pt_free,
):
    side, n, na, nb = cfg
    rows = x_ref.shape[0]
    half = rows // 2
    pieces = out.shape[1]
    dp, tp = lax.axis_index("dp"), lax.axis_index("tp")
    ring_a, ring_b, partner = neighbours(tp, side)
    rings = (ring_a, ring_b)

    def to(t):
        return dict(device_id=(dp, t), device_id_type=MESH)

    barrier = pltpu.get_barrier_semaphore()
    for t in (*ring_a, *ring_b, partner):
        pl.semaphore_signal(barrier, inc=1, **to(t))

    loads = [pltpu.make_async_copy(s, d, w_sem.at[i]) for i, (s, d) in enumerate(((wg_ref, wg), (wu_ref, wu), (wd_ref, wd)))]
    for c in loads:
        c.start()
    run[0] = jnp.zeros_like(run[0])
    pl.semaphore_wait(barrier, 5)

    def span(r):
        return pl.ds(r * half, half)

    def gather(d, r, src=None):
        return pltpu.make_async_remote_copy(
            (xg_ref.at[d, span(r)] if src is None else src.at[span(r)]), xg_ref.at[d + 1, span(r)],
            ag_send.at[d, r], ag_recv.at[d + 1, r], **to(rings[r][0]),
        )

    def share(d, src=None):
        return pltpu.make_async_remote_copy(
            xg_ref.at[d] if src is None else src, xp_ref.at[d], xp_send.at[d], xp_recv.at[d], **to(partner)
        )

    def load_own(d):
        return pltpu.make_async_copy(xg_ref.at[d], xv.at[1], xv_sem.at[1])

    def load_partner(d):
        return pltpu.make_async_copy(xp_ref.at[d], xv.at[0], xv_sem.at[0])

    def pass_sum(s, p, r):
        return pltpu.make_async_remote_copy(
            out.at[s, p, span(r)], run.at[1 - s, p, span(r)], run_send.at[s, p, r], run_recv.at[1 - s, p, r], **to(rings[r][0])
        )

    def got_sum(s, p, r):
        return pltpu.make_async_remote_copy(
            out.at[s, p, span(r)], run.at[s, p, span(r)], run_send.at[s, p, r], run_recv.at[s, p, r], **to(rings[r][0])
        )

    def pass_term(s, p):
        return pltpu.make_async_remote_copy(outp.at[s, p], pt.at[s, p], pt_send.at[s, p], pt_recv.at[s, p], **to(partner))

    def write_y(p):
        return pltpu.make_async_copy(out.at[1, p], y_ref.at[:, pl.ds(pl.multiple_of(p * nb, nb), nb)], y_sem.at[p])

    def up(slot):
        @pl.loop(0, hid.shape[1] // na)
        def _(i):
            c = pl.ds(pl.multiple_of(i * na, na), na)
            gate = jnp.dot(xv[slot], wg[:, c], preferred_element_type=F32)
            up = jnp.dot(xv[slot], wu[:, c], preferred_element_type=F32)
            hid[:, c] = (jax.nn.silu(gate) * up).astype(BF16)

    def down(p):
        c = pl.ds(pl.multiple_of(p * nb, nb), nb)
        return jnp.dot(hid[...], wd[:, c], preferred_element_type=F32)

    for r in range(2):
        gather(0, r, x_ref).start()
    share(n, x_ref).start()
    for r in range(2):
        gather(0, r).wait_recv()
        gather(1, r).start()
    share(1).start()
    load_own(1).start()
    share(1).wait_recv()
    load_partner(1).start()
    for c in loads:
        c.wait()

    @pl.loop(0, n)
    def _(q):
        d = q + 1
        s = q % 2
        load_partner(0).wait()
        up(0)

        @pl.when(d + 1 < n)
        def _():
            for r in range(2):
                gather(d, r).wait_recv()

            @pl.when(d + 2 < n)
            def _():
                for r in range(2):
                    gather(d + 1, r).start()

            share(d + 1).start()

        @pl.when(q >= 2)
        def _():
            pl.semaphore_wait(pt_free, 1)

        @pl.loop(0, pieces)
        def _(p):
            @pl.when(q >= 2)
            def _():
                pass_term(s, p).wait_send()

            outp[s, p] = down(p).astype(BF16)
            pass_term(s, p).start()

        load_own(0).wait()
        up(1)

        @pl.when(d + 1 < n)
        def _():
            load_own(d + 1).start()

        @pl.when(d + 1 == n)
        def _():
            pltpu.make_async_copy(x_ref, xv.at[1], xv_sem.at[1]).start()

        @pl.when(d < n)
        def _():
            share(d + 1, x_ref).wait_recv()
            load_partner(d + 1).start()

        @pl.when((q >= 1) & (d < n))
        def _():
            for r in range(2):
                pl.semaphore_wait(run_free.at[r], 1)

        @pl.loop(0, pieces)
        def _(p):
            @pl.when(q >= 2)
            def _():
                for r in range(2):
                    pass_sum(s, p, r).wait_send()

            @pl.when(q >= 1)
            def _():
                for r in range(2):
                    got_sum(s, p, r).wait_recv()

            pass_term(s, p).wait_recv()
            out[s, p] = (down(p) + run[s, p].astype(F32) + pt[s, p].astype(F32)).astype(BF16)

            @pl.when(d < n)
            def _():
                for r in range(2):
                    pass_sum(s, p, r).start()

            @pl.when(d == n)
            def _():
                write_y(p).start()

        @pl.when(q < n - 2)
        def _():
            for r in range(2):
                pl.semaphore_signal(run_free.at[r], inc=1, **to(rings[r][1]))
            pl.semaphore_signal(pt_free, inc=1, **to(partner))

    @pl.loop(0, pieces)
    def _(p):
        write_y(p).wait()
        for s in range(2):
            pass_term(s, p).wait_send()
        for r in range(2):
            pass_sum(0, p, r).wait_send()

    @pl.loop(0, n - 1)
    def _(d):
        for r in range(2):
            gather(d, r).wait_send()
        share(d + 1).wait_send()

    share(n, x_ref).wait_send()


def solution(mesh):
    group = mesh.shape["tp"]
    n = group // 2
    side = math.isqrt(n)

    def step(x, w_gate, w_up, w_down):
        rows, depth = x.shape
        width = w_gate.shape[1]
        na, nb = width // 2, depth // 5
        pieces = depth // nb
        hbm = pl.BlockSpec(memory_space=pltpu.HBM)
        part = pltpu.VMEM((2, pieces, rows, nb), BF16)
        dma = pltpu.SemaphoreType.DMA
        flops = 6 * group * rows * depth * width
        y, _, _ = pl.pallas_call(
            functools.partial(kernel, (side, n, na, nb)),
            out_shape=(
                jax.ShapeDtypeStruct((rows, depth), BF16),
                jax.ShapeDtypeStruct((n, rows, depth), BF16),
                jax.ShapeDtypeStruct((n + 1, rows, depth), BF16),
            ),
            in_specs=[hbm] * 4,
            out_specs=(hbm,) * 3,
            scratch_shapes=[
                pltpu.VMEM((depth, width), BF16),
                pltpu.VMEM((depth, width), BF16),
                pltpu.VMEM((width, depth), BF16),
                pltpu.VMEM((2, rows, depth), BF16),
                pltpu.VMEM((rows, width), BF16),
                part, part, part, part,
                dma((3,)), dma((2,)), dma((pieces,)),
                dma((n, 2)), dma((n, 2)), dma((n + 1,)), dma((n + 1,)),
                dma((2, pieces, 2)), dma((2, pieces, 2)), dma((2, pieces)), dma((2, pieces)),
                pltpu.SemaphoreType.REGULAR((2,)), pltpu.SemaphoreType.REGULAR,
            ],
            compiler_params=pltpu.CompilerParams(
                collective_id=0, has_side_effects=True, vmem_limit_bytes=63 * 2**20
            ),
            cost_estimate=pl.CostEstimate(flops=flops, bytes_accessed=4 * group * rows * depth, transcendentals=0),
            name="mlp",
        )(x, w_gate, w_up, w_down)
        return y

    return jax.shard_map(
        step,
        mesh=mesh,
        in_specs=(P(("dp", "tp"), None), P(None, "tp"), P(None, "tp"), P("tp", None)),
        out_specs=P(("dp", "tp"), None),
        check_vma=False,
    )
```

time: 794 us -> 399 us (0.50)
  waiting for transfers between devices: 521 us -> 0 us
  Pallas kernels: 0 us -> 395 us
  matrix products: 259 us -> 0 us
  between operations: 13.4 us -> 0.01 us
    pallas_call x0 -> x1, Pallas kernels: none -> 395 us  [step(): pl.pallas_call(functools.partial(kernel, (side, n, na, nb)), out_shape=(j...]
    unnamed x3 -> x0, waiting for transfers between devices: 304 us -> none
    dot_general x3 -> x0, matrix products: 259 us -> none  [the longest x1 87.6 us: step(): up = jnp.dot(rows, w_up, preferred_element_type=jnp.float32)]
    all_gather x1 -> x0, waiting for transfers between devices: 217 us -> none  [step(): rows = lax.all_gather(x, 'tp', axis=0, tiled=True)]
  transfers between devices with their start and end apart: 2 -> 0, of which waited for: 2 -> 0; matrix products, arithmetic and copies ran while one was open for 0% -> 0% of each run, Pallas kernels for 0% -> 0%
where the time goes in v1:
time: 399 us; the launch traced here: 398 us
  Pallas kernels  395 us (99%)
    pallas_call x1, Pallas kernels, step(): pl.pallas_call(functools.partial(kernel, (side, n, na, nb)), out_shape=(j...  395 us

profile of v1, /device:TPU:96, one launch (start us, length us, event | category | flops | bytes accessed | tf_op | source)
XLA Modules:
  0.0 398.4 jit_solution(5882592137159613982)
XLA Ops:
  0.0 395.2 %mlp.1 = (bf16[224,5120]{1,0:T(8,128)(2,1)}, bf16[16,224,5120]{2,1,0:T(8,128)(2,1)}, bf16[17,224,5120]{2,1,0:T(8,128)(2,1)}) custom-call(bf16[224,5120]{1,0:T(8,128)(2,1)} %x_ref.1, bf16[5120,1024]{1,0:T(8,128)(2,1)} %wg_ref.1, bf16[5120,1024]{1,0:T(8,128)(2,1)} %wu_ref.1, bf16[1024,5120]{1,0:T(8,128)(2,1)} %wd_ref.1), custom_call_target="tpu_custom_call" | custom-call | flops 225485783040 | bytes 146800640 | tf_op jit(solution)/shard_map/mlp/pallas_call | solution.py:234
  395.2 3.2 copy.6

commit v2 on v0

v2 whole, which is shorter than its diff:
```python
import functools
import math

import jax
import jax.numpy as jnp
from jax import lax
from jax.experimental import pallas as pl
from jax.experimental.pallas import tpu as pltpu
from jax.sharding import PartitionSpec as P

MESH = pl.DeviceIdType.MESH
BF16 = jnp.bfloat16
F32 = jnp.float32
PARTS = 2
PIECES = 5
SPARE = 4


def neighbours(tp, side):
    core, chip = tp % 2, tp // 2
    x, y = chip // side, chip % side
    last = ((x + y) % side + 1) // side
    first = (side - (x + y) % side) // side

    def at(u, v):
        return (u * side + v) * 2 + core

    a = (at((x + last) % side, (y + 1 - last) % side), at((x + side - first) % side, (y + side - 1 + first) % side))
    b = (at((x + 1 - last) % side, (y + last) % side), at((x + side - 1 + first) % side, (y + side - first) % side))
    turn = lambda p: (p[0] + core * (p[1] - p[0]), p[1] + core * (p[0] - p[1]))
    return turn(a), turn(b), tp + 1 - 2 * core


def kernel(
    n, side,
    x_ref, wg_ref, wu_ref, wd_ref,
    y_ref, xg_ref, xp_ref,
    wg, wu, wd, xo, xp, hid, run, pt, out, outp,
    w_sem, xo_sem, xp_sem, y_sem, ag_send, ag_recv, sh_send, sh_recv, run_send, run_recv, pt_send, pt_recv, run_free, pt_free,
):
    rows, depth = x_ref.shape
    half = rows // 2
    na, nb, nc = hid.shape[2] // PARTS, depth // PIECES, depth // PARTS
    dp, tp = lax.axis_index("dp"), lax.axis_index("tp")
    ring_a, ring_b, partner = neighbours(tp, side)
    rings = (ring_a, ring_b)

    def to(t):
        return dict(device_id=(dp, t), device_id_type=MESH)

    def span(r):
        return pl.ds(r * half, half)

    def cols(i, size):
        return pl.ds(pl.multiple_of(i * size, size), size)

    def gather(d, g, r, src=None):
        return pltpu.make_async_remote_copy(
            (xg_ref.at[d] if src is None else src).at[span(r), cols(g, nc)], xg_ref.at[d + 1, span(r), cols(g, nc)],
            ag_send.at[d, g, r], ag_recv.at[d + 1, g, r], **to(rings[r][0]),
        )

    def share(d, g, src=None):
        return pltpu.make_async_remote_copy(
            (xg_ref.at[d] if src is None else src).at[:, cols(g, nc)], xp_ref.at[d, :, cols(g, nc)],
            sh_send.at[d, g], sh_recv.at[d, g], **to(partner),
        )

    def load_own(d, src=None):
        return pltpu.make_async_copy(xg_ref.at[d] if src is None else src, xo.at[d % 2], xo_sem.at[d % 2])

    def load_partner(d):
        return pltpu.make_async_copy(xp_ref.at[d], xp, xp_sem)

    def pass_sum(q, p, r):
        s, t = q % 2, (q + 1) % 2
        return pltpu.make_async_remote_copy(
            out.at[s, p, span(r)], run.at[t, p, span(r)], run_send.at[s, p, r], run_recv.at[t, p, r], **to(rings[r][0])
        )

    def pass_term(s, t, p):
        return pltpu.make_async_remote_copy(outp.at[s, p], pt.at[t, p], pt_send.at[s, p], pt_recv.at[t, p], **to(partner))

    def write_y(p):
        return pltpu.make_async_copy(out.at[0, p], y_ref.at[:, cols(p, nb)], y_sem.at[p])

    def up(x, slot, between=None):
        @pl.loop(0, PARTS)
        def _(i):
            c = cols(i, na)
            gate = jnp.dot(x[...], wg[:, c], preferred_element_type=F32)
            up = jnp.dot(x[...], wu[:, c], preferred_element_type=F32)
            hid[slot, :, c] = (jax.nn.silu(gate) * up).astype(BF16)
            if between is not None:
                between(i)

    def down(slot, p):
        return jnp.dot(hid[slot], wd[:, cols(p, nb)], preferred_element_type=F32)

    barrier = pltpu.get_barrier_semaphore()
    for t in (*ring_a, *ring_b, partner):
        pl.semaphore_signal(barrier, inc=1, **to(t))
    loads = [pltpu.make_async_copy(s, d, w_sem.at[i]) for i, (s, d) in enumerate(((wg_ref, wg), (wu_ref, wu), (wd_ref, wd)))]
    for c in loads:
        c.start()
    pl.semaphore_wait(barrier, 5)

    for g in range(PARTS):
        for r in range(2):
            gather(0, g, r, x_ref).start()
    for g in range(PARTS):
        share(0, g, x_ref).start()
    run[1] = jnp.zeros_like(run[1])
    for g in range(PARTS):
        share(0, g, x_ref).wait_recv()
    load_partner(0).start()
    loads[0].wait()
    loads[1].wait()

    @pl.loop(0, n + 1)
    def _(q):
        s = q % 2

        @pl.when(q < n)
        def _():
            load_partner(0).wait()

            def between(g):
                @pl.when(q + 1 < n)
                def _():
                    for r in range(2):
                        gather(q, g, r).wait_recv()

                    @pl.when(q + 2 < n)
                    def _():
                        for r in range(2):
                            gather(q + 1, g, r).start()

                    share(q + 1, g).start()

            up(xp, 3, between)

            @pl.when(q + 1 < n)
            def _():
                load_own(q + 1).start()

            @pl.when(q == 0)
            def _():
                loads[2].wait()

            @pl.when(q >= 3)
            def _():
                pl.semaphore_wait(pt_free, 1)

            t = jnp.where(q == 0, 2, s)

            @pl.loop(0, PIECES)
            def _(p):
                @pl.when(q >= 2)
                def _():
                    pass_term(s, 0, p).wait_send()

                outp[s, p] = down(3, p).astype(BF16)
                pass_term(s, t, p).start()

        @pl.when(q == SPARE)
        def _():
            load_own(0, x_ref).start()

        @pl.when((q >= 1) & (q < n - 1))
        def _():
            @pl.loop(q + jnp.minimum(q // 3, 1), q + 1 + jnp.minimum(q // 2, 1))
            def _(u):
                load_own(u, x_ref).wait()
                up(xo.at[u % 2], u % 2)

        @pl.when(q == SPARE)
        def _():
            load_own(0, x_ref).wait()
            up(xo.at[0], 2)

        @pl.when(q + 1 < n)
        def _():
            for g in range(PARTS):
                share(q + 1, g).wait_recv()
            load_partner(q + 1).start()

        @pl.when(q >= 1)
        def _():
            t = jnp.where(q == n, 2, s)

            @pl.when((q >= 2) & (q < n))
            def _():
                for r in range(2):
                    pl.semaphore_wait(run_free.at[r], 1)

            @pl.loop(0, PIECES)
            def _(p):
                @pl.when(q >= 3)
                def _():
                    for r in range(2):
                        pass_sum(q, p, r).wait_send()

                @pl.when(q >= 2)
                def _():
                    for r in range(2):
                        pass_sum(q + 1, p, r).wait_recv()

                pass_term(s, t, p).wait_recv()
                out[s, p] = (down(t, p) + run[s, p].astype(F32) + pt[t, p].astype(F32)).astype(BF16)

                @pl.when(q < n)
                def _():
                    for r in range(2):
                        pass_sum(q, p, r).start()

                @pl.when(q == n)
                def _():
                    write_y(p).start()

            @pl.when(q < n - 1)
            def _():
                for r in range(2):
                    pl.semaphore_signal(run_free.at[r], inc=1, **to(rings[r][1]))

            @pl.when(q < n - 2)
            def _():
                pl.semaphore_signal(pt_free, inc=1, **to(partner))

    @pl.loop(0, PIECES)
    def _(p):
        write_y(p).wait()
        for s in range(2):
            pass_term(s, 0, p).wait_send()
        for r in range(2):
            pass_sum(n - 1, p, r).wait_send()

    @pl.loop(0, n)
    def _(d):
        for g in range(PARTS):
            share(d, g).wait_send()

            @pl.when(d < n - 1)
            def _():
                for r in range(2):
                    gather(d, g, r).wait_send()


def solution(mesh):
    n = mesh.shape["tp"] // 2
    side = math.isqrt(n)

    def step(x, w_gate, w_up, w_down):
        rows, depth = x.shape
        width = w_gate.shape[1]
        hbm = pl.BlockSpec(memory_space=pltpu.HBM)
        dma, flag = pltpu.SemaphoreType.DMA, pltpu.SemaphoreType.REGULAR

        def sums(slots):
            return pltpu.VMEM((slots, PIECES, rows, depth // PIECES), BF16)

        y, _, _ = pl.pallas_call(
            functools.partial(kernel, n, side),
            out_shape=(
                jax.ShapeDtypeStruct((rows, depth), BF16),
                jax.ShapeDtypeStruct((n, rows, depth), BF16),
                jax.ShapeDtypeStruct((n, rows, depth), BF16),
            ),
            in_specs=[hbm] * 4,
            out_specs=(hbm,) * 3,
            scratch_shapes=[
                pltpu.VMEM((depth, width), BF16),
                pltpu.VMEM((depth, width), BF16),
                pltpu.VMEM((width, depth), BF16),
                pltpu.VMEM((2, rows, depth), BF16),
                pltpu.VMEM((rows, depth), BF16),
                pltpu.VMEM((4, rows, width), BF16),
                sums(2), sums(3), sums(2), sums(2),
                dma((3,)), dma((2,)), dma, dma((PIECES,)),
                dma((n, PARTS, 2)), dma((n, PARTS, 2)), dma((n, PARTS)), dma((n, PARTS)),
                dma((2, PIECES, 2)), dma((2, PIECES, 2)), dma((2, PIECES)), dma((3, PIECES)),
                flag((2,)), flag,
            ],
            compiler_params=pltpu.CompilerParams(collective_id=0, has_side_effects=True, vmem_limit_bytes=63 * 2**20),
            cost_estimate=pl.CostEstimate(
                flops=6 * 2 * n * rows * depth * width, bytes_accessed=8 * 2 * n * rows * depth, transcendentals=0
            ),
            name="mlp",
        )(x, w_gate, w_up, w_down)
        return y

    return jax.shard_map(
        step,
        mesh=mesh,
        in_specs=(P(("dp", "tp"), None), P(None, "tp"), P(None, "tp"), P("tp", None)),
        out_specs=P(("dp", "tp"), None),
        check_vma=False,
    )
```

time: 794 us -> 385 us (0.48)
  waiting for transfers between devices: 521 us -> 0 us
  Pallas kernels: 0 us -> 382 us
  matrix products: 259 us -> 0 us
  between operations: 13.4 us -> 0.01 us
    pallas_call x0 -> x1, Pallas kernels: none -> 382 us  [step(): pl.pallas_call(functools.partial(kernel, n, side), out_shape=(jax.ShapeDt...]
    unnamed x3 -> x0, waiting for transfers between devices: 304 us -> none
    dot_general x3 -> x0, matrix products: 259 us -> none  [the longest x1 87.6 us: step(): up = jnp.dot(rows, w_up, preferred_element_type=jnp.float32)]
    all_gather x1 -> x0, waiting for transfers between devices: 217 us -> none  [step(): rows = lax.all_gather(x, 'tp', axis=0, tiled=True)]
  transfers between devices with their start and end apart: 2 -> 0, of which waited for: 2 -> 0; matrix products, arithmetic and copies ran while one was open for 0% -> 0% of each run, Pallas kernels for 0% -> 0%
where the time goes in v2:
time: 385 us
  Pallas kernels  382 us (99%)
    pallas_call x1, Pallas kernels, step(): pl.pallas_call(functools.partial(kernel, n, side), out_shape=(jax.ShapeDt...  382 us

profile of v2, /device:TPU:96, one launch (start us, length us, event | category | flops | bytes accessed | tf_op | source)
XLA Modules:
  0.0 385.0 jit_solution(9091644508012581861)
XLA Ops:
  0.0 381.9 %mlp.1 = (bf16[224,5120]{1,0:T(8,128)(2,1)}, bf16[16,224,5120]{2,1,0:T(8,128)(2,1)}, bf16[16,224,5120]{2,1,0:T(8,128)(2,1)}) custom-call(bf16[224,5120]{1,0:T(8,128)(2,1)} %x_ref.1, bf16[5120,1024]{1,0:T(8,128)(2,1)} %wg_ref.1, bf16[5120,1024]{1,0:T(8,128)(2,1)} %wu_ref.1, bf16[1024,5120]{1,0:T(8,128)(2,1)} %wd_ref.1), custom_call_target="tpu_custom_call" | custom-call | flops 225485783040 | bytes 293601280 | tf_op jit(solution)/shard_map/mlp/pallas_call | solution.py:262
  381.9 3.2 copy.6

commit v3 on v2

--- a/solution.py
+++ b/solution.py
@@ -34,9 +34,9 @@
 def kernel(
     n, side,
     x_ref, wg_ref, wu_ref, wd_ref,
-    y_ref, xg_ref, xp_ref,
+    y_ref, xg_ref, xp_ref, pt0_ref,
     wg, wu, wd, xo, xp, hid, run, pt, out, outp,
-    w_sem, xo_sem, xp_sem, y_sem, ag_send, ag_recv, sh_send, sh_recv, run_send, run_recv, pt_send, pt_recv, run_free, pt_free,
+    w_sem, xo_sem, xp_sem, pt0_sem, ag_send, ag_recv, sh_send, sh_recv, run_send, run_recv, pt_send, pt_recv, run_free, pt_free,
 ):
     rows, depth = x_ref.shape
     half = rows // 2
@@ -67,22 +67,25 @@
         )
 
     def load_own(d, src=None):
-        return pltpu.make_async_copy(xg_ref.at[d] if src is None else src, xo.at[d % 2], xo_sem.at[d % 2])
+        return pltpu.make_async_copy(xg_ref.at[d] if src is None else src, xo, xo_sem)
 
     def load_partner(d):
         return pltpu.make_async_copy(xp_ref.at[d], xp, xp_sem)
 
     def pass_sum(q, p, r):
-        s, t = q % 2, (q + 1) % 2
+        t = (q + 1) % 2
         return pltpu.make_async_remote_copy(
-            out.at[s, p, span(r)], run.at[t, p, span(r)], run_send.at[s, p, r], run_recv.at[t, p, r], **to(rings[r][0])
+            out.at[p, span(r)], run.at[t, p, span(r)], run_send.at[p, r], run_recv.at[t, p, r], **to(rings[r][0])
         )
 
-    def pass_term(s, t, p):
-        return pltpu.make_async_remote_copy(outp.at[s, p], pt.at[t, p], pt_send.at[s, p], pt_recv.at[t, p], **to(partner))
-
-    def write_y(p):
-        return pltpu.make_async_copy(out.at[0, p], y_ref.at[:, cols(p, nb)], y_sem.at[p])
+    def pass_term(t, p):
+        return pltpu.make_async_remote_copy(outp.at[p], pt.at[t, p], pt_send.at[p], pt_recv.at[t, p], **to(partner))
+
+    def pass_first(p):
+        return pltpu.make_async_remote_copy(outp.at[p], pt0_ref.at[p], pt_send.at[p], pt_recv.at[2, p], **to(partner))
+
+    def load_first():
+        return pltpu.make_async_copy(pt0_ref, pt.at[0], pt0_sem)
 
     def up(x, slot, between=None):
         @pl.loop(0, PARTS)
@@ -140,7 +143,7 @@
 
             up(xp, 3, between)
 
-            @pl.when(q + 1 < n)
+            @pl.when((q == 0) | (q >= 3) & (q + 1 < n))
             def _():
                 load_own(q + 1).start()
 
@@ -151,33 +154,39 @@
             @pl.when(q >= 3)
             def _():
                 pl.semaphore_wait(pt_free, 1)
-
-            t = jnp.where(q == 0, 2, s)
 
             @pl.loop(0, PIECES)
             def _(p):
-                @pl.when(q >= 2)
-                def _():
-                    pass_term(s, 0, p).wait_send()
-
-                outp[s, p] = down(3, p).astype(BF16)
-                pass_term(s, t, p).start()
-
-        @pl.when(q == SPARE)
-        def _():
-            load_own(0, x_ref).start()
+                @pl.when(q >= 1)
+                def _():
+                    pass_term(0, p).wait_send()
+
+                outp[p] = down(3, p).astype(BF16)
+
+                @pl.when(q == 0)
+                def _():
+                    pass_first(p).start()
+
+                @pl.when(q >= 1)
+                def _():
+                    pass_term(s, p).start()
 
         @pl.when((q >= 1) & (q < n - 1))
         def _():
             @pl.loop(q + jnp.minimum(q // 3, 1), q + 1 + jnp.minimum(q // 2, 1))
             def _(u):
-                load_own(u, x_ref).wait()
-                up(xo.at[u % 2], u % 2)
+                load_own(0, x_ref).wait()
+                up(xo, u % 2)
+
+                @pl.when(u <= 2)
+                def _():
+                    load_own(u + 1).start()
 
         @pl.when(q == SPARE)
         def _():
+            load_own(0, x_ref).start()
             load_own(0, x_ref).wait()
-            up(xo.at[0], 2)
+            up(xo, 2)
 
         @pl.when(q + 1 < n)
         def _():
@@ -187,7 +196,11 @@
 
         @pl.when(q >= 1)
         def _():
-            t = jnp.where(q == n, 2, s)
+            h = jnp.where(q == n, 2, s)
+
+            @pl.when(q == n)
+            def _():
+                load_first().wait()
 
             @pl.when((q >= 2) & (q < n))
             def _():
@@ -196,7 +209,7 @@
 
             @pl.loop(0, PIECES)
             def _(p):
-                @pl.when(q >= 3)
+                @pl.when((q >= 2) & (q < n))
                 def _():
                     for r in range(2):
                         pass_sum(q, p, r).wait_send()
@@ -206,17 +219,21 @@
                     for r in range(2):
                         pass_sum(q + 1, p, r).wait_recv()
 
-                pass_term(s, t, p).wait_recv()
-                out[s, p] = (down(t, p) + run[s, p].astype(F32) + pt[t, p].astype(F32)).astype(BF16)
-
                 @pl.when(q < n)
                 def _():
+                    pass_term(s, p).wait_recv()
+
+                total = (down(h, p) + run[s, p].astype(F32) + pt[s, p].astype(F32)).astype(BF16)
+
+                @pl.when(q < n)
+                def _():
+                    out[p] = total
                     for r in range(2):
                         pass_sum(q, p, r).start()
 
                 @pl.when(q == n)
                 def _():
-                    write_y(p).start()
+                    y_ref[:, cols(p, nb)] = total
 
             @pl.when(q < n - 1)
             def _():
@@ -227,11 +244,15 @@
             def _():
                 pl.semaphore_signal(pt_free, inc=1, **to(partner))
 
+            @pl.when(q == n - 2)
+            def _():
+                for p in range(PIECES):
+                    pass_first(p).wait_recv()
+                load_first().start()
+
     @pl.loop(0, PIECES)
     def _(p):
-        write_y(p).wait()
-        for s in range(2):
-            pass_term(s, 0, p).wait_send()
+        pass_term(0, p).wait_send()
         for r in range(2):
             pass_sum(n - 1, p, r).wait_send()
 
@@ -256,32 +277,33 @@
         hbm = pl.BlockSpec(memory_space=pltpu.HBM)
         dma, flag = pltpu.SemaphoreType.DMA, pltpu.SemaphoreType.REGULAR
 
-        def sums(slots):
-            return pltpu.VMEM((slots, PIECES, rows, depth // PIECES), BF16)
-
-        y, _, _ = pl.pallas_call(
+        def sums(*slots):
+            return pltpu.VMEM((*slots, PIECES, rows, depth // PIECES), BF16)
+
+        y, *_ = pl.pallas_call(
             functools.partial(kernel, n, side),
             out_shape=(
                 jax.ShapeDtypeStruct((rows, depth), BF16),
                 jax.ShapeDtypeStruct((n, rows, depth), BF16),
                 jax.ShapeDtypeStruct((n, rows, depth), BF16),
+                jax.ShapeDtypeStruct((PIECES, rows, depth // PIECES), BF16),
             ),
             in_specs=[hbm] * 4,
-            out_specs=(hbm,) * 3,
+            out_specs=(pl.BlockSpec(memory_space=pltpu.VMEM), hbm, hbm, hbm),
             scratch_shapes=[
                 pltpu.VMEM((depth, width), BF16),
                 pltpu.VMEM((depth, width), BF16),
                 pltpu.VMEM((width, depth), BF16),
-                pltpu.VMEM((2, rows, depth), BF16),
+                pltpu.VMEM((rows, depth), BF16),
                 pltpu.VMEM((rows, depth), BF16),
                 pltpu.VMEM((4, rows, width), BF16),
-                sums(2), sums(3), sums(2), sums(2),
-                dma((3,)), dma((2,)), dma, dma((PIECES,)),
+                sums(2), sums(2), sums(), sums(),
+                dma((3,)), dma, dma, dma,
                 dma((n, PARTS, 2)), dma((n, PARTS, 2)), dma((n, PARTS)), dma((n, PARTS)),
-                dma((2, PIECES, 2)), dma((2, PIECES, 2)), dma((2, PIECES)), dma((3, PIECES)),
+                dma((PIECES, 2)), dma((2, PIECES, 2)), dma((PIECES,)), dma((3, PIECES)),
                 flag((2,)), flag,
             ],
-            compiler_params=pltpu.CompilerParams(collective_id=0, has_side_effects=True, vmem_limit_bytes=63 * 2**20),
+            compiler_params=pltpu.CompilerParams(collective_id=0, has_side_effects=True, vmem_limit_bytes=int(51.6 * 2**20)),
             cost_estimate=pl.CostEstimate(
                 flops=6 * 2 * n * rows * depth * width, bytes_accessed=8 * 2 * n * rows * depth, transcendentals=0
             ),

time: 385 us -> 383 us (level)
  no operation moved by 1% of the time
where the time goes in v3:
time: 383 us; the launch traced here: 382 us
  Pallas kernels  381 us (99%)
    pallas_call x1, Pallas kernels, step(): pl.pallas_call(functools.partial(kernel, n, side), out_shape=(jax.ShapeDt...  381 us

profile of v3, /device:TPU:96, one launch (start us, length us, event | category | flops | bytes accessed | tf_op | source)
XLA Modules:
  0.0 382.5 jit_solution(5558647867926794378)
XLA Ops:
  0.0 381.1 %mlp.1 = (bf16[224,5120]{1,0:T(8,128)(2,1)S(1)}, bf16[16,224,5120]{2,1,0:T(8,128)(2,1)}, bf16[16,224,5120]{2,1,0:T(8,128)(2,1)}, bf16[5,224,1024]{2,1,0:T(8,128)(2,1)}) custom-call(bf16[224,5120]{1,0:T(8,128)(2,1)} %x_ref.1, bf16[5120,1024]{1,0:T(8,128)(2,1)} %wg_ref.1, bf16[5120,1024]{1,0:T(8,128)(2,1)} %wu_ref.1, bf16[1024,5120]{1,0:T(8,128)(2,1)} %wd_ref.1), custom_call_target="tpu_custom_call" | custom-call | flops 225485783040 | bytes 293601280 | tf_op jit(solution)/shard_map/mlp/pallas_call | solution.py:283
  381.1 1.4 copy.6

commit v4 on v3

--- a/solution.py
+++ b/solution.py
@@ -87,26 +87,40 @@
     def load_first():
         return pltpu.make_async_copy(pt0_ref, pt.at[0], pt0_sem)
 
-    def up(x, slot, between=None):
-        @pl.loop(0, PARTS)
-        def _(i):
-            c = cols(i, na)
-            gate = jnp.dot(x[...], wg[:, c], preferred_element_type=F32)
-            up = jnp.dot(x[...], wu[:, c], preferred_element_type=F32)
-            hid[slot, :, c] = (jax.nn.silu(gate) * up).astype(BF16)
-            if between is not None:
-                between(i)
+    def up(x, slot, i):
+        c = cols(i, na)
+        gate = jnp.dot(x[...], wg[:, c], preferred_element_type=F32)
+        up = jnp.dot(x[...], wu[:, c], preferred_element_type=F32)
+        hid[slot, :, c] = (jax.nn.silu(gate) * up).astype(BF16)
+
+    def advance(d, g):
+        @pl.when(d < n)
+        def _():
+            for r in range(2):
+                gather(d - 1, g, r).wait_recv()
+
+            @pl.when(d + 1 < n)
+            def _():
+                for r in range(2):
+                    gather(d, g, r).start()
+
+            share(d, g).start()
+
+    def await_partner(d):
+        for g in range(PARTS):
+            share(d, g).wait_recv()
+        load_partner(d).start()
 
     def down(slot, p):
         return jnp.dot(hid[slot], wd[:, cols(p, nb)], preferred_element_type=F32)
 
     barrier = pltpu.get_barrier_semaphore()
-    for t in (*ring_a, *ring_b, partner):
+    for t in (ring_a[1], ring_b[1], partner):
         pl.semaphore_signal(barrier, inc=1, **to(t))
     loads = [pltpu.make_async_copy(s, d, w_sem.at[i]) for i, (s, d) in enumerate(((wg_ref, wg), (wu_ref, wu), (wd_ref, wd)))]
     for c in loads:
         c.start()
-    pl.semaphore_wait(barrier, 5)
+    pl.semaphore_wait(barrier, 3)
 
     for g in range(PARTS):
         for r in range(2):
@@ -126,24 +140,19 @@
 
         @pl.when(q < n)
         def _():
-            load_partner(0).wait()
-
-            def between(g):
-                @pl.when(q + 1 < n)
-                def _():
-                    for r in range(2):
-                        gather(q, g, r).wait_recv()
-
-                    @pl.when(q + 2 < n)
-                    def _():
-                        for r in range(2):
-                            gather(q + 1, g, r).start()
-
-                    share(q + 1, g).start()
-
-            up(xp, 3, between)
-
-            @pl.when((q == 0) | (q >= 3) & (q + 1 < n))
+            @pl.when(q < n - 1)
+            def _():
+                load_partner(0).wait()
+
+                @pl.loop(0, PARTS)
+                def _(i):
+                    up(xp, 3, i)
+
+                    @pl.when((q != 1) | (i == 0))
+                    def _():
+                        advance(q + 1, jnp.where(q == 1, 1, i))
+
+            @pl.when((q != 2) & (q + 1 < n))
             def _():
                 load_own(q + 1).start()
 
@@ -171,28 +180,37 @@
                 def _():
                     pass_term(s, p).start()
 
-        @pl.when((q >= 1) & (q < n - 1))
-        def _():
-            @pl.loop(q + jnp.minimum(q // 3, 1), q + 1 + jnp.minimum(q // 2, 1))
+        @pl.when((q != 1) & (q < n - 1))
+        def _():
+            @pl.loop(jnp.where(q == 2, 2, q + 1), q + 2)
             def _(u):
                 load_own(0, x_ref).wait()
-                up(xo, u % 2)
-
-                @pl.when(u <= 2)
-                def _():
-                    load_own(u + 1).start()
+
+                @pl.loop(0, jnp.where(q == n - 2, 1, PARTS))
+                def _(i):
+                    up(xo, u % 2, i)
+
+                    @pl.when((u == 1) & (i == 0))
+                    def _():
+                        advance(2, 0)
+                        await_partner(1)
+
+                @pl.when(u == 2)
+                def _():
+                    load_own(3).start()
 
         @pl.when(q == SPARE)
         def _():
             load_own(0, x_ref).start()
             load_own(0, x_ref).wait()
-            up(xo, 2)
-
-        @pl.when(q + 1 < n)
-        def _():
-            for g in range(PARTS):
-                share(q + 1, g).wait_recv()
-            load_partner(q + 1).start()
+
+            @pl.loop(0, PARTS)
+            def _(i):
+                up(xo, 2, i)
+
+        @pl.when((q >= 1) & (q + 1 < n))
+        def _():
+            await_partner(q + 1)
 
         @pl.when(q >= 1)
         def _():
@@ -201,39 +219,66 @@
             @pl.when(q == n)
             def _():
                 load_first().wait()
+
+                @pl.loop(0, PIECES)
+                def _(p):
+                    pass_term(0, p).wait_send()
+
+                @pl.loop(0, n)
+                def _(d):
+                    for g in range(PARTS):
+                        share(d, g).wait_send()
+
+                        @pl.when(d < n - 1)
+                        def _():
+                            for r in range(2):
+                                gather(d, g, r).wait_send()
 
             @pl.when((q >= 2) & (q < n))
             def _():
                 for r in range(2):
                     pl.semaphore_wait(run_free.at[r], 1)
 
-            @pl.loop(0, PIECES)
-            def _(p):
-                @pl.when((q >= 2) & (q < n))
-                def _():
-                    for r in range(2):
-                        pass_sum(q, p, r).wait_send()
-
-                @pl.when(q >= 2)
-                def _():
-                    for r in range(2):
-                        pass_sum(q + 1, p, r).wait_recv()
-
-                @pl.when(q < n)
-                def _():
-                    pass_term(s, p).wait_recv()
-
-                total = (down(h, p) + run[s, p].astype(F32) + pt[s, p].astype(F32)).astype(BF16)
-
-                @pl.when(q < n)
-                def _():
-                    out[p] = total
-                    for r in range(2):
-                        pass_sum(q, p, r).start()
-
-                @pl.when(q == n)
-                def _():
-                    y_ref[:, cols(p, nb)] = total
+            tail = q == n - 2
+
+            @pl.loop(0, jnp.where(tail, 3, 1))
+            def _(k):
+                @pl.loop(jnp.where(tail, jnp.maximum(2 * k - 1, 0), 0), jnp.where(tail, 2 * k + 1, PIECES))
+                def _(p):
+                    @pl.when(q >= 2)
+                    def _():
+                        for r in range(2):
+                            pass_sum(q, p, r).wait_send()
+
+                    @pl.when(q >= 2)
+                    def _():
+                        for r in range(2):
+                            pass_sum(q + 1, p, r).wait_recv()
+
+                    @pl.when(q < n)
+                    def _():
+                        pass_term(s, p).wait_recv()
+
+                    total = (down(h, p) + run[s, p].astype(F32) + pt[s, p].astype(F32)).astype(BF16)
+
+                    @pl.when(q < n)
+                    def _():
+                        out[p] = total
+                        for r in range(2):
+                            pass_sum(q, p, r).start()
+
+                    @pl.when(q == n)
+                    def _():
+                        y_ref[:, cols(p, nb)] = total
+
+                @pl.when(tail & (k == 0))
+                def _():
+                    up(xo, (n - 1) % 2, 1)
+                    load_partner(0).wait()
+
+                @pl.when(tail & (k > 0))
+                def _():
+                    up(xp, 3, k - 1)
 
             @pl.when(q < n - 1)
             def _():
@@ -249,22 +294,6 @@
                 for p in range(PIECES):
                     pass_first(p).wait_recv()
                 load_first().start()
-
-    @pl.loop(0, PIECES)
-    def _(p):
-        pass_term(0, p).wait_send()
-        for r in range(2):
-            pass_sum(n - 1, p, r).wait_send()
-
-    @pl.loop(0, n)
-    def _(d):
-        for g in range(PARTS):
-            share(d, g).wait_send()
-
-            @pl.when(d < n - 1)
-            def _():
-                for r in range(2):
-                    gather(d, g, r).wait_send()
 
 
 def solution(mesh):
@@ -303,7 +332,7 @@
                 dma((PIECES, 2)), dma((2, PIECES, 2)), dma((PIECES,)), dma((3, PIECES)),
                 flag((2,)), flag,
             ],
-            compiler_params=pltpu.CompilerParams(collective_id=0, has_side_effects=True, vmem_limit_bytes=int(51.6 * 2**20)),
+            compiler_params=pltpu.CompilerParams(collective_id=0, has_side_effects=True, vmem_limit_bytes=int(51.75 * 2**20)),
             cost_estimate=pl.CostEstimate(
                 flops=6 * 2 * n * rows * depth * width, bytes_accessed=8 * 2 * n * rows * depth, transcendentals=0
             ),

time: 383 us -> 382 us (level)
  no operation moved by 1% of the time
where the time goes in v4:
time: 382 us
  Pallas kernels  380 us (99%)
    pallas_call x1, Pallas kernels, step(): pl.pallas_call(functools.partial(kernel, n, side), out_shape=(jax.ShapeDt...  380 us

profile of v4, /device:TPU:96, one launch (start us, length us, event | category | flops | bytes accessed | tf_op | source)
XLA Modules:
  0.0 381.6 jit_solution(13375900829226772118)
XLA Ops:
  0.0 380.2 %mlp.1 = (bf16[224,5120]{1,0:T(8,128)(2,1)S(1)}, bf16[16,224,5120]{2,1,0:T(8,128)(2,1)}, bf16[16,224,5120]{2,1,0:T(8,128)(2,1)}, bf16[5,224,1024]{2,1,0:T(8,128)(2,1)}) custom-call(bf16[224,5120]{1,0:T(8,128)(2,1)} %x_ref.1, bf16[5120,1024]{1,0:T(8,128)(2,1)} %wg_ref.1, bf16[5120,1024]{1,0:T(8,128)(2,1)} %wu_ref.1, bf16[1024,5120]{1,0:T(8,128)(2,1)} %wd_ref.1), custom_call_target="tpu_custom_call" | custom-call | flops 225485783040 | bytes 293601280 | tf_op jit(solution)/shard_map/mlp/pallas_call | solution.py:312
  380.2 1.4 copy.6

commit v5 on v4

--- a/solution.py
+++ b/solution.py
@@ -148,13 +148,9 @@
                 def _(i):
                     up(xp, 3, i)
 
-                    @pl.when((q != 1) | (i == 0))
+                    @pl.when((q == 0) | (q == 1) & (i == 0))
                     def _():
                         advance(q + 1, jnp.where(q == 1, 1, i))
-
-            @pl.when((q != 2) & (q + 1 < n))
-            def _():
-                load_own(q + 1).start()
 
             @pl.when(q == 0)
             def _():
@@ -179,6 +175,15 @@
                 @pl.when(q >= 1)
                 def _():
                     pass_term(s, p).start()
+
+            @pl.when(q >= 2)
+            def _():
+                for g in range(PARTS):
+                    advance(q + 1, g)
+
+            @pl.when((q != 2) & (q + 1 < n))
+            def _():
+                load_own(q + 1).start()
 
         @pl.when((q != 1) & (q < n - 1))
         def _():

time: 382 us -> 381 us (level)
  no operation moved by 1% of the time
where the time goes in v5:
time: 381 us; the launch traced here: 380 us
  Pallas kernels  379 us (99%)
    pallas_call x1, Pallas kernels, step(): pl.pallas_call(functools.partial(kernel, n, side), out_shape=(jax.ShapeDt...  379 us

profile of v5, /device:TPU:96, one launch (start us, length us, event | category | flops | bytes accessed | tf_op | source)
XLA Modules:
  0.0 380.3 jit_solution(6442880460440765453)
XLA Ops:
  0.0 378.9 %mlp.1 = (bf16[224,5120]{1,0:T(8,128)(2,1)S(1)}, bf16[16,224,5120]{2,1,0:T(8,128)(2,1)}, bf16[16,224,5120]{2,1,0:T(8,128)(2,1)}, bf16[5,224,1024]{2,1,0:T(8,128)(2,1)}) custom-call(bf16[224,5120]{1,0:T(8,128)(2,1)} %x_ref.1, bf16[5120,1024]{1,0:T(8,128)(2,1)} %wg_ref.1, bf16[5120,1024]{1,0:T(8,128)(2,1)} %wu_ref.1, bf16[1024,5120]{1,0:T(8,128)(2,1)} %wd_ref.1), custom_call_target="tpu_custom_call" | custom-call | flops 225485783040 | bytes 293601280 | tf_op jit(solution)/shard_map/mlp/pallas_call | solution.py:317
  378.9 1.4 copy.6
